TPU v7x, 32 devices: a whole 2x2x4 slice. The times are simulated.
32 devices in a mesh: row: 8 (over z, core), col: 4 (over y, x).
Axes of the slice: x: 2, y: 2, z: 4, core: 2. Of those that a mesh axis runs over, the one named last changes fastest.
Arguments:
- gradient: float32 [8192, 28672], P('row', 'col'), may hold values from -100 to 100
- residual: float32 [8192, 28672], P('row', 'col'), may hold values from -3 to 3
- q_init: float32 [4, 28672], P(None, 'col'), may hold values from -5 to 5
Outputs:
- q_factor: float32 [4, 28672], P(None, 'col')
- new_residual: float32 [8192, 28672], P('row', 'col')
All inputs are finite; a program needn't handle non-finite values.
Results may differ from a plain program's by a relative error of at most 0.00012.
Values sent between devices are 32-bit elements; how exact they have to be, the bound alone decides.
A program may use at most 128 MiB of HBM per device.

v0:
```python
import jax
import jax.numpy as jnp
from jax import lax
from jax.sharding import PartitionSpec as P

ITERS = 16


def sum_over_cols(partial_value):
    return lax.psum(partial_value, "col")


def shards(gradient, residual, q_init):
    highest = lax.Precision.HIGHEST
    merged = gradient + residual

    def iterate(step_index, carry):
        q_current, p_previous = carry
        p_partial = lax.dot_general(
            q_current,
            merged,
            (((1,), (1,)), ((), ())),
            precision=highest,
            preferred_element_type=jnp.float32,
        )
        p_factor = sum_over_cols(p_partial)
        gram_part = lax.dot_general(
            p_factor,
            p_factor,
            (((1,), (1,)), ((), ())),
            precision=highest,
            preferred_element_type=jnp.float32,
        )
        cross_part = jnp.dot(
            p_factor, merged, precision=highest, preferred_element_type=jnp.float32
        )
        gram, cross = lax.psum((gram_part, cross_part), "row")
        factor_low = jnp.linalg.cholesky(gram)
        p_basis = jax.scipy.linalg.solve_triangular(factor_low, p_factor, lower=True)
        q_next = jax.scipy.linalg.solve_triangular(factor_low, cross, lower=True)
        return (q_next, p_basis)

    start = (q_init, jnp.zeros((q_init.shape[0], merged.shape[0]), jnp.float32))
    q_factor, p_basis = lax.fori_loop(0, ITERS, iterate, start)
    approx = lax.dot_general(
        p_basis,
        q_factor,
        (((0,), (0,)), ((), ())),
        precision=highest,
        preferred_element_type=jnp.float32,
    )
    return (q_factor, merged - approx)


def solution(mesh):
    in_specs = (P("row", "col"), P("row", "col"), P(None, "col"))
    out_specs = (P(None, "col"), P("row", "col"))
    return jax.shard_map(shards, mesh=mesh, in_specs=in_specs, out_specs=out_specs, check_vma=False)
```

profile of v0, /device:TPU:1, one launch (start us, length us, event | category | flops | bytes accessed | tf_op | source)
XLA Modules:
  0.0 1912.1 jit_solution(13343573732617844287)
XLA Ops:
  7.2 30.9 %add.27 = f32[1024,7168]{1,0:T(8,128)} add(f32[1024,7168]{1,0:T(8,128)} %param.5, f32[1024,7168]{1,0:T(8,128)} %param.6) | non-fusion elementwise | flops 7340032 | bytes 88080384 | tf_op jit(solution)/shard_map/add | solution.py:15
  38.1 1837.0 %while.12 = (s32[]{:T(128)}, f32[4,7168]{1,0:T(4,128)S(1)}, f32[4,1024]{1,0:T(4,128)}, f32[1024,7168]{1,0:T(8,128)}, s32[]{:T(128)}) while((s32[]{:T(128)}, f32[4,7168]{1,0:T(4,128)S(1)}, f32[4,1024]{1,0:T(4,128)}, f32[1024,7168]{1,0:T(8,128)}, s32[]{:T(128)}) %tuple.27), condition=%wide.region_6.7_spmd, body=%wide.region_0.6_spmd.sunk | while | flops 706445440 | bytes 59982788 | solution.py:44
  38.1 27.1 %fusion.46 = f32[4,1024]{1,0:T(4,128)S(1)} fusion(f32[4,7168]{1,0:T(4,128)S(1)} %get-tuple-element.63, f32[1024,7168]{1,0:T(8,128)} %get-tuple-element.70), kind=kOutput, calls=%fused_computation.13.clone.1 | convolution fusion | flops 352321536 | bytes 29491200 | tf_op jit(solution)/shard_map/while/body/eval_jaxpr/dot_general | solution.py:19
  117.1 35.7 %all-reduce.2.cloned.1.call-done = f32[4,7168]{1,0:T(4,128)} async-done(((f32[4,7168]{1,0:T(4,128)}), f32[4,7168]{1,0:T(4,128)}) %all-reduce.2.cloned.1.call-update) | async-done | bytes 114704 | tf_op jit(solution)/shard_map/while/body/eval_jaxpr/psum | solution.py:37
  154.1 27.1 %fusion.46 = f32[4,1024]{1,0:T(4,128)S(1)} fusion(f32[4,7168]{1,0:T(4,128)S(1)} %get-tuple-element.63, f32[1024,7168]{1,0:T(8,128)} %get-tuple-element.70), kind=kOutput, calls=%fused_computation.13.clone.1 | convolution fusion | flops 352321536 | bytes 29491200 | tf_op jit(solution)/shard_map/while/body/eval_jaxpr/dot_general | solution.py:19
  231.7 35.8 %all-reduce.2.cloned.1.call-done = f32[4,7168]{1,0:T(4,128)} async-done(((f32[4,7168]{1,0:T(4,128)}), f32[4,7168]{1,0:T(4,128)}) %all-reduce.2.cloned.1.call-update) | async-done | bytes 114704 | tf_op jit(solution)/shard_map/while/body/eval_jaxpr/psum | solution.py:37
  268.9 27.1 %fusion.46 = f32[4,1024]{1,0:T(4,128)S(1)} fusion(f32[4,7168]{1,0:T(4,128)S(1)} %get-tuple-element.63, f32[1024,7168]{1,0:T(8,128)} %get-tuple-element.70), kind=kOutput, calls=%fused_computation.13.clone.1 | convolution fusion | flops 352321536 | bytes 29491200 | tf_op jit(solution)/shard_map/while/body/eval_jaxpr/dot_general | solution.py:19
  346.5 35.8 %all-reduce.2.cloned.1.call-done = f32[4,7168]{1,0:T(4,128)} async-done(((f32[4,7168]{1,0:T(4,128)}), f32[4,7168]{1,0:T(4,128)}) %all-reduce.2.cloned.1.call-update) | async-done | bytes 114704 | tf_op jit(solution)/shard_map/while/body/eval_jaxpr/psum | solution.py:37
  383.7 27.1 %fusion.46 = f32[4,1024]{1,0:T(4,128)S(1)} fusion(f32[4,7168]{1,0:T(4,128)S(1)} %get-tuple-element.63, f32[1024,7168]{1,0:T(8,128)} %get-tuple-element.70), kind=kOutput, calls=%fused_computation.13.clone.1 | convolution fusion | flops 352321536 | bytes 29491200 | tf_op jit(solution)/shard_map/while/body/eval_jaxpr/dot_general | solution.py:19
  461.3 35.8 %all-reduce.2.cloned.1.call-done = f32[4,7168]{1,0:T(4,128)} async-done(((f32[4,7168]{1,0:T(4,128)}), f32[4,7168]{1,0:T(4,128)}) %all-reduce.2.cloned.1.call-update) | async-done | bytes 114704 | tf_op jit(solution)/shard_map/while/body/eval_jaxpr/psum | solution.py:37
  498.4 27.1 %fusion.46 = f32[4,1024]{1,0:T(4,128)S(1)} fusion(f32[4,7168]{1,0:T(4,128)S(1)} %get-tuple-element.63, f32[1024,7168]{1,0:T(8,128)} %get-tuple-element.70), kind=kOutput, calls=%fused_computation.13.clone.1 | convolution fusion | flops 352321536 | bytes 29491200 | tf_op jit(solution)/shard_map/while/body/eval_jaxpr/dot_general | solution.py:19
  576.0 35.8 %all-reduce.2.cloned.1.call-done = f32[4,7168]{1,0:T(4,128)} async-done(((f32[4,7168]{1,0:T(4,128)}), f32[4,7168]{1,0:T(4,128)}) %all-reduce.2.cloned.1.call-update) | async-done | bytes 114704 | tf_op jit(solution)/shard_map/while/body/eval_jaxpr/psum | solution.py:37
  613.1 27.1 %fusion.46 = f32[4,1024]{1,0:T(4,128)S(1)} fusion(f32[4,7168]{1,0:T(4,128)S(1)} %get-tuple-element.63, f32[1024,7168]{1,0:T(8,128)} %get-tuple-element.70), kind=kOutput, calls=%fused_computation.13.clone.1 | convolution fusion | flops 352321536 | bytes 29491200 | tf_op jit(solution)/shard_map/while/body/eval_jaxpr/dot_general | solution.py:19
  690.7 35.8 %all-reduce.2.cloned.1.call-done = f32[4,7168]{1,0:T(4,128)} async-done(((f32[4,7168]{1,0:T(4,128)}), f32[4,7168]{1,0:T(4,128)}) %all-reduce.2.cloned.1.call-update) | async-done | bytes 114704 | tf_op jit(solution)/shard_map/while/body/eval_jaxpr/psum | solution.py:37
  727.9 27.1 %fusion.46 = f32[4,1024]{1,0:T(4,128)S(1)} fusion(f32[4,7168]{1,0:T(4,128)S(1)} %get-tuple-element.63, f32[1024,7168]{1,0:T(8,128)} %get-tuple-element.70), kind=kOutput, calls=%fused_computation.13.clone.1 | convolution fusion | flops 352321536 | bytes 29491200 | tf_op jit(solution)/shard_map/while/body/eval_jaxpr/dot_general | solution.py:19
  805.4 35.8 %all-reduce.2.cloned.1.call-done = f32[4,7168]{1,0:T(4,128)} async-done(((f32[4,7168]{1,0:T(4,128)}), f32[4,7168]{1,0:T(4,128)}) %all-reduce.2.cloned.1.call-update) | async-done | bytes 114704 | tf_op jit(solution)/shard_map/while/body/eval_jaxpr/psum | solution.py:37
  842.6 27.1 %fusion.46 = f32[4,1024]{1,0:T(4,128)S(1)} fusion(f32[4,7168]{1,0:T(4,128)S(1)} %get-tuple-element.63, f32[1024,7168]{1,0:T(8,128)} %get-tuple-element.70), kind=kOutput, calls=%fused_computation.13.clone.1 | convolution fusion | flops 352321536 | bytes 29491200 | tf_op jit(solution)/shard_map/while/body/eval_jaxpr/dot_general | solution.py:19
  920.2 35.8 %all-reduce.2.cloned.1.call-done = f32[4,7168]{1,0:T(4,128)} async-done(((f32[4,7168]{1,0:T(4,128)}), f32[4,7168]{1,0:T(4,128)}) %all-reduce.2.cloned.1.call-update) | async-done | bytes 114704 | tf_op jit(solution)/shard_map/while/body/eval_jaxpr/psum | solution.py:37
  957.3 27.1 %fusion.46 = f32[4,1024]{1,0:T(4,128)S(1)} fusion(f32[4,7168]{1,0:T(4,128)S(1)} %get-tuple-element.63, f32[1024,7168]{1,0:T(8,128)} %get-tuple-element.70), kind=kOutput, calls=%fused_computation.13.clone.1 | convolution fusion | flops 352321536 | bytes 29491200 | tf_op jit(solution)/shard_map/while/body/eval_jaxpr/dot_general | solution.py:19
  1034.9 35.8 %all-reduce.2.cloned.1.call-done = f32[4,7168]{1,0:T(4,128)} async-done(((f32[4,7168]{1,0:T(4,128)}), f32[4,7168]{1,0:T(4,128)}) %all-reduce.2.cloned.1.call-update) | async-done | bytes 114704 | tf_op jit(solution)/shard_map/while/body/eval_jaxpr/psum | solution.py:37
  1072.1 27.1 %fusion.46 = f32[4,1024]{1,0:T(4,128)S(1)} fusion(f32[4,7168]{1,0:T(4,128)S(1)} %get-tuple-element.63, f32[1024,7168]{1,0:T(8,128)} %get-tuple-element.70), kind=kOutput, calls=%fused_computation.13.clone.1 | convolution fusion | flops 352321536 | bytes 29491200 | tf_op jit(solution)/shard_map/while/body/eval_jaxpr/dot_general | solution.py:19
  1149.7 35.8 %all-reduce.2.cloned.1.call-done = f32[4,7168]{1,0:T(4,128)} async-done(((f32[4,7168]{1,0:T(4,128)}), f32[4,7168]{1,0:T(4,128)}) %all-reduce.2.cloned.1.call-update) | async-done | bytes 114704 | tf_op jit(solution)/shard_map/while/body/eval_jaxpr/psum | solution.py:37
  1186.8 27.1 %fusion.46 = f32[4,1024]{1,0:T(4,128)S(1)} fusion(f32[4,7168]{1,0:T(4,128)S(1)} %get-tuple-element.63, f32[1024,7168]{1,0:T(8,128)} %get-tuple-element.70), kind=kOutput, calls=%fused_computation.13.clone.1 | convolution fusion | flops 352321536 | bytes 29491200 | tf_op jit(solution)/shard_map/while/body/eval_jaxpr/dot_general | solution.py:19
  1264.4 35.8 %all-reduce.2.cloned.1.call-done = f32[4,7168]{1,0:T(4,128)} async-done(((f32[4,7168]{1,0:T(4,128)}), f32[4,7168]{1,0:T(4,128)}) %all-reduce.2.cloned.1.call-update) | async-done | bytes 114704 | tf_op jit(solution)/shard_map/while/body/eval_jaxpr/psum | solution.py:37
  1379.1 35.8 %all-reduce.2.cloned.1.call-done = f32[4,7168]{1,0:T(4,128)} async-done(((f32[4,7168]{1,0:T(4,128)}), f32[4,7168]{1,0:T(4,128)}) %all-reduce.2.cloned.1.call-update) | async-done | bytes 114704 | tf_op jit(solution)/shard_map/while/body/eval_jaxpr/psum | solution.py:37
  1416.2 27.1 %fusion.46 = f32[4,1024]{1,0:T(4,128)S(1)} fusion(f32[4,7168]{1,0:T(4,128)S(1)} %get-tuple-element.63, f32[1024,7168]{1,0:T(8,128)} %get-tuple-element.70), kind=kOutput, calls=%fused_computation.13.clone.1 | convolution fusion | flops 352321536 | bytes 29491200 | tf_op jit(solution)/shard_map/while/body/eval_jaxpr/dot_general | solution.py:19
  1493.8 35.8 %all-reduce.2.cloned.1.call-done = f32[4,7168]{1,0:T(4,128)} async-done(((f32[4,7168]{1,0:T(4,128)}), f32[4,7168]{1,0:T(4,128)}) %all-reduce.2.cloned.1.call-update) | async-done | bytes 114704 | tf_op jit(solution)/shard_map/while/body/eval_jaxpr/psum | solution.py:37
  1608.6 35.8 %all-reduce.2.cloned.1.call-done = f32[4,7168]{1,0:T(4,128)} async-done(((f32[4,7168]{1,0:T(4,128)}), f32[4,7168]{1,0:T(4,128)}) %all-reduce.2.cloned.1.call-update) | async-done | bytes 114704 | tf_op jit(solution)/shard_map/while/body/eval_jaxpr/psum | solution.py:37
  1645.7 27.1 %fusion.46 = f32[4,1024]{1,0:T(4,128)S(1)} fusion(f32[4,7168]{1,0:T(4,128)S(1)} %get-tuple-element.63, f32[1024,7168]{1,0:T(8,128)} %get-tuple-element.70), kind=kOutput, calls=%fused_computation.13.clone.1 | convolution fusion | flops 352321536 | bytes 29491200 | tf_op jit(solution)/shard_map/while/body/eval_jaxpr/dot_general | solution.py:19
  1723.3 35.8 %all-reduce.2.cloned.1.call-done = f32[4,7168]{1,0:T(4,128)} async-done(((f32[4,7168]{1,0:T(4,128)}), f32[4,7168]{1,0:T(4,128)}) %all-reduce.2.cloned.1.call-update) | async-done | bytes 114704 | tf_op jit(solution)/shard_map/while/body/eval_jaxpr/psum | solution.py:37
  1838.0 35.8 %all-reduce.2.cloned.1.call-done = f32[4,7168]{1,0:T(4,128)} async-done(((f32[4,7168]{1,0:T(4,128)}), f32[4,7168]{1,0:T(4,128)}) %all-reduce.2.cloned.1.call-update) | async-done | bytes 114704 | tf_op jit(solution)/shard_map/while/body/eval_jaxpr/psum | solution.py:37
  1875.1 30.4 %convolution_subtract_fusion = f32[1024,7168]{1,0:T(8,128)} fusion(f32[1024,7168]{1,0:T(8,128)} %get-tuple-element.73, f32[4,1024]{1,0:T(4,128)} %get-tuple-element.25, f32[4,7168]{1,0:T(4,128)S(1)} %get-tuple-element.22), kind=kOutput, calls=%fused_computation.12 | convolution fusion | flops 359661568 | bytes 58851328 | tf_op jit(solution)/shard_map/dot_general | solution.py:45
  (248 shorter events, 911.7 us)
Async XLA Ops:
  7.2 31.0 %copy-start.1 = (f32[4,7168]{1,0:T(4,128)S(1)}, f32[4,7168]{1,0:T(4,128)}, u32[]{:S(2)}) copy-start(f32[4,7168]{1,0:T(4,128)} %param.7) | copy-start | bytes 344068
  38.1 114.7 %all-reduce.2.cloned.1.call-start = ((), (), s32[]{:S(2)}) async-start(), calls=%async_computation | async-start | bytes 229376 | tf_op jit(solution)/shard_map/while/body/eval_jaxpr/psum | solution.py:37
  154.1 113.5 %all-reduce.2.cloned.1.call-start = ((), (), s32[]{:S(2)}) async-start(), calls=%async_computation | async-start | bytes 229376 | tf_op jit(solution)/shard_map/while/body/eval_jaxpr/psum | solution.py:37
  268.9 113.4 %all-reduce.2.cloned.1.call-start = ((), (), s32[]{:S(2)}) async-start(), calls=%async_computation | async-start | bytes 229376 | tf_op jit(solution)/shard_map/while/body/eval_jaxpr/psum | solution.py:37
  383.6 113.4 %all-reduce.2.cloned.1.call-start = ((), (), s32[]{:S(2)}) async-start(), calls=%async_computation | async-start | bytes 229376 | tf_op jit(solution)/shard_map/while/body/eval_jaxpr/psum | solution.py:37
  498.3 113.4 %all-reduce.2.cloned.1.call-start = ((), (), s32[]{:S(2)}) async-start(), calls=%async_computation | async-start | bytes 229376 | tf_op jit(solution)/shard_map/while/body/eval_jaxpr/psum | solution.py:37
  613.1 113.4 %all-reduce.2.cloned.1.call-start = ((), (), s32[]{:S(2)}) async-start(), calls=%async_computation | async-start | bytes 229376 | tf_op jit(solution)/shard_map/while/body/eval_jaxpr/psum | solution.py:37
  727.8 113.4 %all-reduce.2.cloned.1.call-start = ((), (), s32[]{:S(2)}) async-start(), calls=%async_computation | async-start | bytes 229376 | tf_op jit(solution)/shard_map/while/body/eval_jaxpr/psum | solution.py:37
  842.5 113.4 %all-reduce.2.cloned.1.call-start = ((), (), s32[]{:S(2)}) async-start(), calls=%async_computation | async-start | bytes 229376 | tf_op jit(solution)/shard_map/while/body/eval_jaxpr/psum | solution.py:37
  957.3 113.4 %all-reduce.2.cloned.1.call-start = ((), (), s32[]{:S(2)}) async-start(), calls=%async_computation | async-start | bytes 229376 | tf_op jit(solution)/shard_map/while/body/eval_jaxpr/psum | solution.py:37
  1072.0 113.4 %all-reduce.2.cloned.1.call-start = ((), (), s32[]{:S(2)}) async-start(), calls=%async_computation | async-start | bytes 229376 | tf_op jit(solution)/shard_map/while/body/eval_jaxpr/psum | solution.py:37
  1186.7 113.4 %all-reduce.2.cloned.1.call-start = ((), (), s32[]{:S(2)}) async-start(), calls=%async_computation | async-start | bytes 229376 | tf_op jit(solution)/shard_map/while/body/eval_jaxpr/psum | solution.py:37
  1301.5 113.4 %all-reduce.2.cloned.1.call-start = ((), (), s32[]{:S(2)}) async-start(), calls=%async_computation | async-start | bytes 229376 | tf_op jit(solution)/shard_map/while/body/eval_jaxpr/psum | solution.py:37
  1416.2 113.4 %all-reduce.2.cloned.1.call-start = ((), (), s32[]{:S(2)}) async-start(), calls=%async_computation | async-start | bytes 229376 | tf_op jit(solution)/shard_map/while/body/eval_jaxpr/psum | solution.py:37
  1530.9 113.4 %all-reduce.2.cloned.1.call-start = ((), (), s32[]{:S(2)}) async-start(), calls=%async_computation | async-start | bytes 229376 | tf_op jit(solution)/shard_map/while/body/eval_jaxpr/psum | solution.py:37
  1645.7 113.4 %all-reduce.2.cloned.1.call-start = ((), (), s32[]{:S(2)}) async-start(), calls=%async_computation | async-start | bytes 229376 | tf_op jit(solution)/shard_map/while/body/eval_jaxpr/psum | solution.py:37
  1760.4 113.4 %all-reduce.2.cloned.1.call-start = ((), (), s32[]{:S(2)}) async-start(), calls=%async_computation | async-start | bytes 229376 | tf_op jit(solution)/shard_map/while/body/eval_jaxpr/psum | solution.py:37
  1875.1 30.4 %copy-start = (f32[4,7168]{1,0:T(4,128)}, f32[4,7168]{1,0:T(4,128)S(1)}, u32[]{:S(2)}) copy-start(f32[4,7168]{1,0:T(4,128)S(1)} %get-tuple-element.22) | copy-start | bytes 344068
Sparse Core Ops, SparseCore 0:
  96.4 56.3 all-reduce.1
  211.5 56.0 all-reduce.1
  326.3 55.9 all-reduce.1
  441.0 55.9 all-reduce.1
  555.7 55.9 all-reduce.1
  670.5 55.9 all-reduce.1
  785.2 55.9 all-reduce.1
  899.9 55.9 all-reduce.1
  1014.7 55.9 all-reduce.1
  1129.4 55.9 all-reduce.1
  1244.1 55.9 all-reduce.1
  1358.9 55.9 all-reduce.1
  1473.6 55.9 all-reduce.1
  1588.3 55.9 all-reduce.1
  1703.0 55.9 all-reduce.1
  1817.8 55.9 all-reduce.1
where the time goes:
time: 1910 us
  matrix products  786 us (41%)
  waiting for transfers between devices  573 us (30%)
  blocking collectives  471 us (25%)
  other arithmetic  65.4 us (3%)
    psum x16, waiting for transfers between devices, iterate(): gram, cross = lax.psum((gram_part, cross_part), 'row')  572 us
    dot_general x16, matrix products, iterate(): lax.dot_general(q_current, merged, (((1,), (1,)), ((), ())), precision=hi...  433 us
    dot_general x16, matrix products, iterate(): jnp.dot(p_factor, merged, precision=highest, preferred_element_type=jnp.f...  286 us
    psum x16, blocking collectives, iterate(): gram, cross = lax.psum((gram_part, cross_part), 'row')  274 us
    psum x16, blocking collectives, sum_over_cols(): return lax.psum(partial_value, 'col')  196 us
  transfers between devices with their start and end apart: 16, of which 16 were waited for; matrix products, arithmetic and copies ran while one was open for 3% of the time, Pallas kernels for 0%

commit v1 on v0

--- a/solution.py
+++ b/solution.py
@@ -1,13 +1,24 @@
+import functools
 import jax
 import jax.numpy as jnp
 from jax import lax
 from jax.sharding import PartitionSpec as P
+from jax.lax import all_gather
 
 ITERS = 16
 
 
+def perform_wall(sample, mesh_name):
+    base_arr = all_gather(sample, mesh_name)
+    piece_out = jnp.sum(base_arr, 0)
+    return piece_out
+
+
+return_all_plate = functools.partial(perform_wall, mesh_name="col")
+
+
 def sum_over_cols(partial_value):
-    return lax.psum(partial_value, "col")
+    return return_all_plate(partial_value)
 
 
 def shards(gradient, residual, q_init):

time: 1910 us -> 1800 us (0.942)
  blocking collectives: 471 us -> 346 us
    psum x16 -> x0, blocking collectives: 196 us -> none  [sum_over_cols(): return lax.psum(partial_value, 'col')]
    all_gather x0 -> x16, blocking collectives: none -> 99.7 us  [perform_wall(): base_arr = all_gather(sample, mesh_name)]
    psum x16, blocking collectives: 274 us -> 246 us  [iterate(): gram, cross = lax.psum((gram_part, cross_part), 'row')]
where the time goes in v1:
time: 1800 us
  matrix products  787 us (44%)
  waiting for transfers between devices  587 us (33%)
  blocking collectives  346 us (19%)
  other arithmetic  65.7 us (4%)
    psum x16, waiting for transfers between devices, iterate(): gram, cross = lax.psum((gram_part, cross_part), 'row')  586 us
    dot_general x16, matrix products, iterate(): lax.dot_general(q_current, merged, (((1,), (1,)), ((), ())), precision=hi...  433 us
    dot_general x16, matrix products, iterate(): jnp.dot(p_factor, merged, precision=highest, preferred_element_type=jnp.f...  287 us
    psum x16, blocking collectives, iterate(): gram, cross = lax.psum((gram_part, cross_part), 'row')  246 us
    all_gather x16, blocking collectives, perform_wall(): base_arr = all_gather(sample, mesh_name)  99.7 us
  transfers between devices with their start and end apart: 16, of which 16 were waited for; matrix products, arithmetic and copies ran while one was open for 3% of the time, Pallas kernels for 0%

profile of v1, /device:TPU:1, one launch (start us, length us, event | category | flops | bytes accessed | tf_op | source)
XLA Modules:
  0.0 1801.9 jit_solution(8929783098629127069)
XLA Ops:
  7.2 30.9 %add.25 = f32[1024,7168]{1,0:T(8,128)} add(f32[1024,7168]{1,0:T(8,128)} %param.5, f32[1024,7168]{1,0:T(8,128)} %param.6) | non-fusion elementwise | flops 7340032 | bytes 88080384 | tf_op jit(solution)/shard_map/add | solution.py:26
  38.1 1726.8 %while.12 = (s32[]{:T(128)}, f32[4,7168]{1,0:T(4,128)S(1)}, f32[4,1024]{1,0:T(4,128)}, f32[1024,7168]{1,0:T(8,128)}, s32[]{:T(128)}, /*index=5*/f32[]{:T(128)}) while((s32[]{:T(128)}, f32[4,7168]{1,0:T(4,128)S(1)}, f32[4,1024]{1,0:T(4,128)}, f32[1024,7168]{1,0:T(8,128)}, s32[]{:T(128)}, /*index=5*/f32[]{:T(128)}) %tuple.27), condition=%wide.region_6.7_spmd, body=%wide.region_0.6_spmd.sunk | while | flops 706453632 | bytes 60113872 | solution.py:55
  38.1 27.1 %convolution_bitcast_fusion.2 = f32[1,4,1024]{2,1,0:T(4,128)S(1)} fusion(f32[4,7168]{1,0:T(4,128)S(1)} %get-tuple-element.64, f32[1024,7168]{1,0:T(8,128)} %get-tuple-element.72), kind=kOutput, calls=%fused_computation.clone.1 | convolution fusion | flops 352321536 | bytes 29491200 | tf_op jit(solution)/shard_map/while/body/eval_jaxpr/dot_general | solution.py:30
  109.3 36.6 %all-reduce.2.cloned.1.call-done = f32[4,7168]{1,0:T(4,128)} async-done(((f32[4,7168]{1,0:T(4,128)}), f32[4,7168]{1,0:T(4,128)}) %all-reduce.2.cloned.1.call-update) | async-done | bytes 114704 | tf_op jit(solution)/shard_map/while/body/eval_jaxpr/psum | solution.py:48
  147.3 27.1 %convolution_bitcast_fusion.2 = f32[1,4,1024]{2,1,0:T(4,128)S(1)} fusion(f32[4,7168]{1,0:T(4,128)S(1)} %get-tuple-element.64, f32[1024,7168]{1,0:T(8,128)} %get-tuple-element.72), kind=kOutput, calls=%fused_computation.clone.1 | convolution fusion | flops 352321536 | bytes 29491200 | tf_op jit(solution)/shard_map/while/body/eval_jaxpr/dot_general | solution.py:30
  217.1 36.6 %all-reduce.2.cloned.1.call-done = f32[4,7168]{1,0:T(4,128)} async-done(((f32[4,7168]{1,0:T(4,128)}), f32[4,7168]{1,0:T(4,128)}) %all-reduce.2.cloned.1.call-update) | async-done | bytes 114704 | tf_op jit(solution)/shard_map/while/body/eval_jaxpr/psum | solution.py:48
  255.1 27.1 %convolution_bitcast_fusion.2 = f32[1,4,1024]{2,1,0:T(4,128)S(1)} fusion(f32[4,7168]{1,0:T(4,128)S(1)} %get-tuple-element.64, f32[1024,7168]{1,0:T(8,128)} %get-tuple-element.72), kind=kOutput, calls=%fused_computation.clone.1 | convolution fusion | flops 352321536 | bytes 29491200 | tf_op jit(solution)/shard_map/while/body/eval_jaxpr/dot_general | solution.py:30
  324.9 36.7 %all-reduce.2.cloned.1.call-done = f32[4,7168]{1,0:T(4,128)} async-done(((f32[4,7168]{1,0:T(4,128)}), f32[4,7168]{1,0:T(4,128)}) %all-reduce.2.cloned.1.call-update) | async-done | bytes 114704 | tf_op jit(solution)/shard_map/while/body/eval_jaxpr/psum | solution.py:48
  363.0 27.1 %convolution_bitcast_fusion.2 = f32[1,4,1024]{2,1,0:T(4,128)S(1)} fusion(f32[4,7168]{1,0:T(4,128)S(1)} %get-tuple-element.64, f32[1024,7168]{1,0:T(8,128)} %get-tuple-element.72), kind=kOutput, calls=%fused_computation.clone.1 | convolution fusion | flops 352321536 | bytes 29491200 | tf_op jit(solution)/shard_map/while/body/eval_jaxpr/dot_general | solution.py:30
  432.8 36.7 %all-reduce.2.cloned.1.call-done = f32[4,7168]{1,0:T(4,128)} async-done(((f32[4,7168]{1,0:T(4,128)}), f32[4,7168]{1,0:T(4,128)}) %all-reduce.2.cloned.1.call-update) | async-done | bytes 114704 | tf_op jit(solution)/shard_map/while/body/eval_jaxpr/psum | solution.py:48
  470.8 27.1 %convolution_bitcast_fusion.2 = f32[1,4,1024]{2,1,0:T(4,128)S(1)} fusion(f32[4,7168]{1,0:T(4,128)S(1)} %get-tuple-element.64, f32[1024,7168]{1,0:T(8,128)} %get-tuple-element.72), kind=kOutput, calls=%fused_computation.clone.1 | convolution fusion | flops 352321536 | bytes 29491200 | tf_op jit(solution)/shard_map/while/body/eval_jaxpr/dot_general | solution.py:30
  540.6 36.7 %all-reduce.2.cloned.1.call-done = f32[4,7168]{1,0:T(4,128)} async-done(((f32[4,7168]{1,0:T(4,128)}), f32[4,7168]{1,0:T(4,128)}) %all-reduce.2.cloned.1.call-update) | async-done | bytes 114704 | tf_op jit(solution)/shard_map/while/body/eval_jaxpr/psum | solution.py:48
  578.6 27.1 %convolution_bitcast_fusion.2 = f32[1,4,1024]{2,1,0:T(4,128)S(1)} fusion(f32[4,7168]{1,0:T(4,128)S(1)} %get-tuple-element.64, f32[1024,7168]{1,0:T(8,128)} %get-tuple-element.72), kind=kOutput, calls=%fused_computation.clone.1 | convolution fusion | flops 352321536 | bytes 29491200 | tf_op jit(solution)/shard_map/while/body/eval_jaxpr/dot_general | solution.py:30
  648.5 36.7 %all-reduce.2.cloned.1.call-done = f32[4,7168]{1,0:T(4,128)} async-done(((f32[4,7168]{1,0:T(4,128)}), f32[4,7168]{1,0:T(4,128)}) %all-reduce.2.cloned.1.call-update) | async-done | bytes 114704 | tf_op jit(solution)/shard_map/while/body/eval_jaxpr/psum | solution.py:48
  686.5 27.1 %convolution_bitcast_fusion.2 = f32[1,4,1024]{2,1,0:T(4,128)S(1)} fusion(f32[4,7168]{1,0:T(4,128)S(1)} %get-tuple-element.64, f32[1024,7168]{1,0:T(8,128)} %get-tuple-element.72), kind=kOutput, calls=%fused_computation.clone.1 | convolution fusion | flops 352321536 | bytes 29491200 | tf_op jit(solution)/shard_map/while/body/eval_jaxpr/dot_general | solution.py:30
  756.3 36.7 %all-reduce.2.cloned.1.call-done = f32[4,7168]{1,0:T(4,128)} async-done(((f32[4,7168]{1,0:T(4,128)}), f32[4,7168]{1,0:T(4,128)}) %all-reduce.2.cloned.1.call-update) | async-done | bytes 114704 | tf_op jit(solution)/shard_map/while/body/eval_jaxpr/psum | solution.py:48
  794.3 27.1 %convolution_bitcast_fusion.2 = f32[1,4,1024]{2,1,0:T(4,128)S(1)} fusion(f32[4,7168]{1,0:T(4,128)S(1)} %get-tuple-element.64, f32[1024,7168]{1,0:T(8,128)} %get-tuple-element.72), kind=kOutput, calls=%fused_computation.clone.1 | convolution fusion | flops 352321536 | bytes 29491200 | tf_op jit(solution)/shard_map/while/body/eval_jaxpr/dot_general | solution.py:30
  864.2 36.7 %all-reduce.2.cloned.1.call-done = f32[4,7168]{1,0:T(4,128)} async-done(((f32[4,7168]{1,0:T(4,128)}), f32[4,7168]{1,0:T(4,128)}) %all-reduce.2.cloned.1.call-update) | async-done | bytes 114704 | tf_op jit(solution)/shard_map/while/body/eval_jaxpr/psum | solution.py:48
  902.2 27.1 %convolution_bitcast_fusion.2 = f32[1,4,1024]{2,1,0:T(4,128)S(1)} fusion(f32[4,7168]{1,0:T(4,128)S(1)} %get-tuple-element.64, f32[1024,7168]{1,0:T(8,128)} %get-tuple-element.72), kind=kOutput, calls=%fused_computation.clone.1 | convolution fusion | flops 352321536 | bytes 29491200 | tf_op jit(solution)/shard_map/while/body/eval_jaxpr/dot_general | solution.py:30
  972.0 36.7 %all-reduce.2.cloned.1.call-done = f32[4,7168]{1,0:T(4,128)} async-done(((f32[4,7168]{1,0:T(4,128)}), f32[4,7168]{1,0:T(4,128)}) %all-reduce.2.cloned.1.call-update) | async-done | bytes 114704 | tf_op jit(solution)/shard_map/while/body/eval_jaxpr/psum | solution.py:48
  1010.0 27.1 %convolution_bitcast_fusion.2 = f32[1,4,1024]{2,1,0:T(4,128)S(1)} fusion(f32[4,7168]{1,0:T(4,128)S(1)} %get-tuple-element.64, f32[1024,7168]{1,0:T(8,128)} %get-tuple-element.72), kind=kOutput, calls=%fused_computation.clone.1 | convolution fusion | flops 352321536 | bytes 29491200 | tf_op jit(solution)/shard_map/while/body/eval_jaxpr/dot_general | solution.py:30
  1079.9 36.7 %all-reduce.2.cloned.1.call-done = f32[4,7168]{1,0:T(4,128)} async-done(((f32[4,7168]{1,0:T(4,128)}), f32[4,7168]{1,0:T(4,128)}) %all-reduce.2.cloned.1.call-update) | async-done | bytes 114704 | tf_op jit(solution)/shard_map/while/body/eval_jaxpr/psum | solution.py:48
  1117.9 27.1 %convolution_bitcast_fusion.2 = f32[1,4,1024]{2,1,0:T(4,128)S(1)} fusion(f32[4,7168]{1,0:T(4,128)S(1)} %get-tuple-element.64, f32[1024,7168]{1,0:T(8,128)} %get-tuple-element.72), kind=kOutput, calls=%fused_computation.clone.1 | convolution fusion | flops 352321536 | bytes 29491200 | tf_op jit(solution)/shard_map/while/body/eval_jaxpr/dot_general | solution.py:30
  1187.7 36.7 %all-reduce.2.cloned.1.call-done = f32[4,7168]{1,0:T(4,128)} async-done(((f32[4,7168]{1,0:T(4,128)}), f32[4,7168]{1,0:T(4,128)}) %all-reduce.2.cloned.1.call-update) | async-done | bytes 114704 | tf_op jit(solution)/shard_map/while/body/eval_jaxpr/psum | solution.py:48
  1225.7 27.1 %convolution_bitcast_fusion.2 = f32[1,4,1024]{2,1,0:T(4,128)S(1)} fusion(f32[4,7168]{1,0:T(4,128)S(1)} %get-tuple-element.64, f32[1024,7168]{1,0:T(8,128)} %get-tuple-element.72), kind=kOutput, calls=%fused_computation.clone.1 | convolution fusion | flops 352321536 | bytes 29491200 | tf_op jit(solution)/shard_map/while/body/eval_jaxpr/dot_general | solution.py:30
  1295.6 36.7 %all-reduce.2.cloned.1.call-done = f32[4,7168]{1,0:T(4,128)} async-done(((f32[4,7168]{1,0:T(4,128)}), f32[4,7168]{1,0:T(4,128)}) %all-reduce.2.cloned.1.call-update) | async-done | bytes 114704 | tf_op jit(solution)/shard_map/while/body/eval_jaxpr/psum | solution.py:48
  1403.4 36.7 %all-reduce.2.cloned.1.call-done = f32[4,7168]{1,0:T(4,128)} async-done(((f32[4,7168]{1,0:T(4,128)}), f32[4,7168]{1,0:T(4,128)}) %all-reduce.2.cloned.1.call-update) | async-done | bytes 114704 | tf_op jit(solution)/shard_map/while/body/eval_jaxpr/psum | solution.py:48
  1511.3 36.7 %all-reduce.2.cloned.1.call-done = f32[4,7168]{1,0:T(4,128)} async-done(((f32[4,7168]{1,0:T(4,128)}), f32[4,7168]{1,0:T(4,128)}) %all-reduce.2.cloned.1.call-update) | async-done | bytes 114704 | tf_op jit(solution)/shard_map/while/body/eval_jaxpr/psum | solution.py:48
  1619.1 36.7 %all-reduce.2.cloned.1.call-done = f32[4,7168]{1,0:T(4,128)} async-done(((f32[4,7168]{1,0:T(4,128)}), f32[4,7168]{1,0:T(4,128)}) %all-reduce.2.cloned.1.call-update) | async-done | bytes 114704 | tf_op jit(solution)/shard_map/while/body/eval_jaxpr/psum | solution.py:48
  1657.1 27.1 %convolution_bitcast_fusion.2 = f32[1,4,1024]{2,1,0:T(4,128)S(1)} fusion(f32[4,7168]{1,0:T(4,128)S(1)} %get-tuple-element.64, f32[1024,7168]{1,0:T(8,128)} %get-tuple-element.72), kind=kOutput, calls=%fused_computation.clone.1 | convolution fusion | flops 352321536 | bytes 29491200 | tf_op jit(solution)/shard_map/while/body/eval_jaxpr/dot_general | solution.py:30
  1727.0 36.7 %all-reduce.2.cloned.1.call-done = f32[4,7168]{1,0:T(4,128)} async-done(((f32[4,7168]{1,0:T(4,128)}), f32[4,7168]{1,0:T(4,128)}) %all-reduce.2.cloned.1.call-update) | async-done | bytes 114704 | tf_op jit(solution)/shard_map/while/body/eval_jaxpr/psum | solution.py:48
  1764.9 30.4 %convolution_subtract_fusion = f32[1024,7168]{1,0:T(8,128)} fusion(f32[1024,7168]{1,0:T(8,128)} %get-tuple-element.76, f32[4,1024]{1,0:T(4,128)} %get-tuple-element.25, f32[4,7168]{1,0:T(4,128)S(1)} %get-tuple-element.22), kind=kOutput, calls=%fused_computation.13 | convolution fusion | flops 359661568 | bytes 58851328 | tf_op jit(solution)/shard_map/dot_general | solution.py:56
  (264 shorter events, 787.4 us)
Async XLA Ops:
  7.2 31.0 %copy-start.1 = (f32[4,7168]{1,0:T(4,128)S(1)}, f32[4,7168]{1,0:T(4,128)}, u32[]{:S(2)}) copy-start(f32[4,7168]{1,0:T(4,128)} %param.7) | copy-start | bytes 344068
  38.1 107.8 %all-reduce.2.cloned.1.call-start = ((), (), s32[]{:S(2)}) async-start(), calls=%async_computation | async-start | bytes 229376 | tf_op jit(solution)/shard_map/while/body/eval_jaxpr/psum | solution.py:48
  147.2 106.5 %all-reduce.2.cloned.1.call-start = ((), (), s32[]{:S(2)}) async-start(), calls=%async_computation | async-start | bytes 229376 | tf_op jit(solution)/shard_map/while/body/eval_jaxpr/psum | solution.py:48
  255.1 106.5 %all-reduce.2.cloned.1.call-start = ((), (), s32[]{:S(2)}) async-start(), calls=%async_computation | async-start | bytes 229376 | tf_op jit(solution)/shard_map/while/body/eval_jaxpr/psum | solution.py:48
  362.9 106.5 %all-reduce.2.cloned.1.call-start = ((), (), s32[]{:S(2)}) async-start(), calls=%async_computation | async-start | bytes 229376 | tf_op jit(solution)/shard_map/while/body/eval_jaxpr/psum | solution.py:48
  470.8 106.5 %all-reduce.2.cloned.1.call-start = ((), (), s32[]{:S(2)}) async-start(), calls=%async_computation | async-start | bytes 229376 | tf_op jit(solution)/shard_map/while/body/eval_jaxpr/psum | solution.py:48
  578.6 106.5 %all-reduce.2.cloned.1.call-start = ((), (), s32[]{:S(2)}) async-start(), calls=%async_computation | async-start | bytes 229376 | tf_op jit(solution)/shard_map/while/body/eval_jaxpr/psum | solution.py:48
  686.4 106.5 %all-reduce.2.cloned.1.call-start = ((), (), s32[]{:S(2)}) async-start(), calls=%async_computation | async-start | bytes 229376 | tf_op jit(solution)/shard_map/while/body/eval_jaxpr/psum | solution.py:48
  794.3 106.5 %all-reduce.2.cloned.1.call-start = ((), (), s32[]{:S(2)}) async-start(), calls=%async_computation | async-start | bytes 229376 | tf_op jit(solution)/shard_map/while/body/eval_jaxpr/psum | solution.py:48
  902.1 106.5 %all-reduce.2.cloned.1.call-start = ((), (), s32[]{:S(2)}) async-start(), calls=%async_computation | async-start | bytes 229376 | tf_op jit(solution)/shard_map/while/body/eval_jaxpr/psum | solution.py:48
  1010.0 106.5 %all-reduce.2.cloned.1.call-start = ((), (), s32[]{:S(2)}) async-start(), calls=%async_computation | async-start | bytes 229376 | tf_op jit(solution)/shard_map/while/body/eval_jaxpr/psum | solution.py:48
  1117.8 106.5 %all-reduce.2.cloned.1.call-start = ((), (), s32[]{:S(2)}) async-start(), calls=%async_computation | async-start | bytes 229376 | tf_op jit(solution)/shard_map/while/body/eval_jaxpr/psum | solution.py:48
  1225.7 106.5 %all-reduce.2.cloned.1.call-start = ((), (), s32[]{:S(2)}) async-start(), calls=%async_computation | async-start | bytes 229376 | tf_op jit(solution)/shard_map/while/body/eval_jaxpr/psum | solution.py:48
  1333.5 106.5 %all-reduce.2.cloned.1.call-start = ((), (), s32[]{:S(2)}) async-start(), calls=%async_computation | async-start | bytes 229376 | tf_op jit(solution)/shard_map/while/body/eval_jaxpr/psum | solution.py:48
  1441.4 106.5 %all-reduce.2.cloned.1.call-start = ((), (), s32[]{:S(2)}) async-start(), calls=%async_computation | async-start | bytes 229376 | tf_op jit(solution)/shard_map/while/body/eval_jaxpr/psum | solution.py:48
  1549.2 106.5 %all-reduce.2.cloned.1.call-start = ((), (), s32[]{:S(2)}) async-start(), calls=%async_computation | async-start | bytes 229376 | tf_op jit(solution)/shard_map/while/body/eval_jaxpr/psum | solution.py:48
  1657.1 106.5 %all-reduce.2.cloned.1.call-start = ((), (), s32[]{:S(2)}) async-start(), calls=%async_computation | async-start | bytes 229376 | tf_op jit(solution)/shard_map/while/body/eval_jaxpr/psum | solution.py:48
  1764.9 30.4 %copy-start = (f32[4,7168]{1,0:T(4,128)}, f32[4,7168]{1,0:T(4,128)S(1)}, u32[]{:S(2)}) copy-start(f32[4,7168]{1,0:T(4,128)S(1)} %get-tuple-element.22) | copy-start | bytes 344068
Sparse Core Ops, SparseCore 0:
  90.4 55.4 all-reduce.1
  198.6 55.1 all-reduce.1
  306.4 55.1 all-reduce.1
  414.3 55.1 all-reduce.1
  522.1 55.1 all-reduce.1
  630.0 55.1 all-reduce.1
  737.8 55.1 all-reduce.1
  845.7 55.1 all-reduce.1
  953.5 55.1 all-reduce.1
  1061.4 55.1 all-reduce.1
  1169.2 55.1 all-reduce.1
  1277.1 55.1 all-reduce.1
  1384.9 55.1 all-reduce.1
  1492.8 55.1 all-reduce.1
  1600.6 55.1 all-reduce.1
  1708.5 55.1 all-reduce.1
